TPU v7x, 32 devices: a whole 2x2x4 slice. The times are simulated.
32 devices in a mesh: gx: 4 (over z), gy: 8 (over y, x, core).
Axes of the slice: x: 2, y: 2, z: 4, core: 2. Of those that a mesh axis runs over, the one named last changes fastest.
Arguments:
- node_coords: float32 [12288, 3, 128], P(('gx', 'gy')), may hold values from -6 to 6
- node_disp: float32 [12288, 3, 128], P(('gx', 'gy')), may hold values from -6 to 6
- qpoints: float32 [8192, 3, 256], P(('gx', 'gy')), may hold values from -6 to 6
- qweights: float32 [8192, 256], P(('gx', 'gy')), may hold values from 0.1 to 2
- qcount: int32 [8192], P(('gx', 'gy')), may hold values from 64 to 256
- sec_block: int32 [8192], P(('gx', 'gy')), may hold values from 0 to 12287, as said below
- pri_block: int32 [8192], P(('gx', 'gy')), may hold values from 0 to 12287, as said below
Outputs:
- gap: float32 [12288, 3, 128], P(('gx', 'gy'))
Inputs may be any that keep to these rules, and one draw needn't show every extreme that they name: `sec_block`: patch b is owned by device b // 384. Among the segments of one device, at most 16 have their secondary patch owned by any one device; in every draw some device owns the secondary patches of exactly 16 segments of every device. `pri_block`: as for sec_block, with primary patches: at most 16 segments of one device name patches of any one owner, and some owner gets exactly 16 from every device.
All inputs are finite; a program needn't handle non-finite values.
Results may differ from a plain program's by a relative error of at most 0.000098.
Values sent between devices are 32-bit elements; how exact they have to be, the bound alone decides.
A program may use at most 64 MiB of HBM per device.

v0:
```python
import functools
import jax
import jax.numpy as jnp
from jax import lax
from jax.experimental import pallas as pl
from jax.experimental.pallas import tpu as pltpu
from jax.sharding import PartitionSpec as P

GROUP = 16
UNROLL = 8


def routing(block_ids, blocks_dev, capacity, slot_count):
    owners = block_ids // blocks_dev
    local_ids = block_ids % blocks_dev
    positions = jnp.arange(block_ids.shape[0], dtype=jnp.int32)
    same_owner = (owners[:, None] == owners[None, :]) & (positions[:, None] > positions[None, :])
    ranks = jnp.sum(same_owner.astype(jnp.int32), axis=1)
    slot_ids = owners * capacity + ranks
    matches = slot_ids[:, None] == jnp.arange(slot_count, dtype=jnp.int32)[None, :]
    request = jnp.sum(jnp.where(matches, local_ids[:, None], 0), axis=0)
    return slot_ids, request


def exchange(x):
    return lax.all_to_all(x, ("gx", "gy"), split_axis=0, concat_axis=0, tiled=True)


def gather_kernel(ids, coords, disp, out):
    comps, _, n = coords.shape

    @pl.loop(0, out.shape[0])
    def _(i):
        for j in range(UNROLL):
            b = ids[i * UNROLL + j]
            for c in range(comps):
                out[i, j : j + 1, c * n : (c + 1) * n] = coords[c, pl.ds(b, 1), :]
                k = comps + c
                out[i, j : j + 1, k * n : (k + 1) * n] = disp[c, pl.ds(b, 1), :]


def gather_rows(ids, coords, disp):
    rows, width = ids.shape[0], 2 * coords.shape[0] * coords.shape[2]
    return pl.pallas_call(
        gather_kernel,
        out_shape=jax.ShapeDtypeStruct((rows // UNROLL, UNROLL, width), jnp.float32),
        in_specs=[
            pl.BlockSpec(memory_space=pltpu.SMEM),
            pl.BlockSpec(memory_space=pltpu.VMEM),
            pl.BlockSpec(memory_space=pltpu.VMEM),
        ],
        out_specs=pl.BlockSpec(memory_space=pltpu.VMEM),
        name="gather_rows",
    )(ids, coords, disp).reshape(rows, width)


def rounded(x):
    return x.astype(jnp.bfloat16).astype(jnp.float32)


def stack_rows(rows, iota):
    out = jnp.zeros(iota.shape, jnp.float32)
    for i, row in rows:
        out = jnp.where(iota == i, row, out)
    return out


def disp_rows(row, n):
    iota = lax.broadcasted_iota(jnp.int32, (8, n), 0)
    u = [row[:, (3 + c) * n : (4 + c) * n] for c in range(3)]
    full = stack_rows([(i + 4 * h, u[i]) for h in range(2) for i in range(3)], iota)
    full = jnp.where((iota == 3) | (iota == 7), 1.0, full)
    both = jnp.where(iota < 4, rounded(full), full - rounded(full)).astype(jnp.bfloat16)
    return jnp.concatenate([both, both], axis=1)


def side(row, feat, n):
    bf, f32 = jnp.bfloat16, jnp.float32
    iota = lax.broadcasted_iota(jnp.int32, (8, n), 0)
    x = [row[:, c * n : (c + 1) * n] for c in range(3)]
    square = 2.0 * (x[0] * x[0] + x[1] * x[1] + x[2] * x[2])
    full = stack_rows(
        [(0, -4.0 * x[0]), (1, -4.0 * x[1]), (2, -4.0 * x[2]), (3, square), (4, 1.0)], iota
    )
    high = rounded(full)
    rest = full - high
    mid = rounded(rest)
    left = jnp.concatenate([high, high, mid, high, rest - mid, mid], axis=0)
    kern = 1.0 / jnp.dot(left.T.astype(bf), feat, preferred_element_type=f32)
    kh = kern.astype(bf)
    kl = (kern - kh.astype(f32)).astype(bf)
    both = jnp.concatenate([kh, kl], axis=0)
    a = jnp.dot(disp_rows(row, n), both, preferred_element_type=f32)
    total = a + pltpu.roll(a, 4, 0)
    inv = 1.0 / total[3:4]
    return both, total * inv, inv


def pri_kernel(slots, nodes, feats, means):
    n = nodes.shape[1] // 6
    for g in range(feats.shape[0]):
        row = nodes[pl.ds(slots[pl.program_id(0) * feats.shape[0] + g], 1), :]
        means[g] = side(row, feats[g], n)[1]


def sec_kernel(slots, nodes, feats, weights, means, parcels):
    n = nodes.shape[1] // 6
    step = pl.program_id(0)

    @pl.when(step == 0)
    def _():
        parcels[...] = jnp.zeros_like(parcels)

    iota = lax.broadcasted_iota(jnp.int32, (8, feats.shape[2]), 0)
    for g in range(feats.shape[0]):
        slot = slots[step * feats.shape[0] + g]
        both, mean, inv = side(nodes[pl.ds(slot, 1), :], feats[g], n)
        gap = (mean - means[g]) * (weights[g : g + 1] * inv)
        high = rounded(gap)
        gap = jnp.where(iota < 4, high, gap - high).astype(jnp.bfloat16)
        c = lax.dot_general(
            gap, both, (((1,), (1,)), ((), ())), preferred_element_type=jnp.float32
        )
        c = c[:, :n] + c[:, n:]
        c = c + pltpu.roll(c, 4, 0)
        parcels[slot] = c[:3]


def cost(segs, points, n):
    return pl.CostEstimate(
        flops=8 * segs * points * n * 16, bytes_accessed=segs * points * 128, transcendentals=0
    )


def pri_means(slots_of, nodes, feats):
    segs, depth, points = feats.shape
    slots, width = nodes.shape
    return pl.pallas_call(
        pri_kernel,
        grid_spec=pltpu.PrefetchScalarGridSpec(
            num_scalar_prefetch=1,
            grid=(segs // GROUP,),
            in_specs=[
                pl.BlockSpec((slots, width), lambda i, *_: (0, 0)),
                pl.BlockSpec((GROUP, depth, points), lambda i, *_: (i, 0, 0)),
            ],
            out_specs=pl.BlockSpec((GROUP, 8, points), lambda i, *_: (i, 0, 0)),
        ),
        out_shape=jax.ShapeDtypeStruct((segs, 8, points), jnp.float32),
        cost_estimate=cost(segs, points, width // 6),
        name="pri_means",
    )(slots_of, nodes, feats)


def coupling(slots_of, nodes, feats, weights, means):
    segs, depth, points = feats.shape
    slots, width = nodes.shape
    n = width // 6
    return pl.pallas_call(
        sec_kernel,
        grid_spec=pltpu.PrefetchScalarGridSpec(
            num_scalar_prefetch=1,
            grid=(segs // GROUP,),
            in_specs=[
                pl.BlockSpec((slots, width), lambda i, *_: (0, 0)),
                pl.BlockSpec((GROUP, depth, points), lambda i, *_: (i, 0, 0)),
                pl.BlockSpec((GROUP, points), lambda i, *_: (i, 0)),
                pl.BlockSpec((GROUP, 8, points), lambda i, *_: (i, 0, 0)),
            ],
            out_specs=pl.BlockSpec((slots, 3, n), lambda i, *_: (0, 0, 0)),
        ),
        out_shape=jax.ShapeDtypeStruct((slots, 3, n), jnp.float32),
        cost_estimate=cost(segs, points, n),
        name="coupling",
    )(slots_of, nodes, feats, weights, means).reshape(slots, 3 * n)


def assemble_kernel(ids, incoming, gap):
    comps, blocks, n = gap.shape
    slots = incoming.shape[0]
    match = lax.broadcasted_iota(jnp.int32, (blocks, slots), 0) == ids[...]
    select = jnp.where(match, 1.0, 0.0).astype(jnp.bfloat16)
    for c in range(comps):
        x = incoming[:, c * n : (c + 1) * n]
        high = rounded(x)
        rest = x - high
        mid = rounded(rest)
        pieces = jnp.concatenate([high, mid, rest - mid], axis=1).astype(jnp.bfloat16)
        y = jnp.dot(select, pieces, preferred_element_type=jnp.float32)
        gap[c] = y[:, :n] + (y[:, n : 2 * n] + y[:, 2 * n :])


def assemble(ids, incoming, blocks, comps):
    n = incoming.shape[1] // comps
    return pl.pallas_call(
        assemble_kernel,
        out_shape=jax.ShapeDtypeStruct((comps, blocks, n), jnp.float32),
        in_specs=[pl.BlockSpec(memory_space=pltpu.VMEM)] * 2,
        out_specs=pl.BlockSpec(memory_space=pltpu.VMEM),
        name="assemble",
    )(ids[None, :], incoming).transpose(1, 0, 2)


def point_features(qpoints):
    square = 1.0 + 2.0 * jnp.sum(qpoints * qpoints, axis=1, keepdims=True)
    ones = jnp.ones_like(square)
    full = jnp.concatenate([qpoints, ones, square, jnp.zeros_like(qpoints)], axis=1)
    high = lax.reduce_precision(full, 8, 7)
    rest = full - high
    mid = lax.reduce_precision(rest, 8, 7)
    low = rest - mid
    return jnp.concatenate([high, mid, high, low, high, mid], axis=1).astype(jnp.bfloat16)


def body(node_coords, node_disp, qpoints, qweights, qcount, sec_block, pri_block):
    devices = lax.axis_size("gx") * lax.axis_size("gy")
    blocks_dev, comps, node_count = node_coords.shape
    seg_count = qpoints.shape[0]
    quad_points = qpoints.shape[2]
    slot_count = 2 * seg_count
    capacity = slot_count // devices
    sec_slots, sec_request = routing(sec_block, blocks_dev, capacity, slot_count)
    pri_slots, pri_request = routing(pri_block, blocks_dev, capacity, slot_count)
    requests = jnp.stack(
        [sec_request.reshape(devices, capacity), pri_request.reshape(devices, capacity)], axis=1
    )
    received = exchange(requests)
    sec_ids = received[:, 0].reshape(slot_count)
    pri_ids = received[:, 1].reshape(slot_count)
    coords = node_coords.transpose(1, 0, 2)
    disp = node_disp.transpose(1, 0, 2)
    pri_nodes = exchange(gather_rows(pri_ids, coords, disp))
    sec_rows, feats, pri_nodes = lax.optimization_barrier(
        (gather_rows(sec_ids, coords, disp), point_features(qpoints), pri_nodes)
    )
    sec_nodes = exchange(sec_rows)
    live = jnp.arange(quad_points, dtype=jnp.int32)[None, :] < qcount[:, None]
    weights = jnp.where(live, qweights, jnp.zeros_like(qweights))
    means = pri_means(pri_slots, pri_nodes, feats)
    parcels = coupling(sec_slots, sec_nodes, feats, weights, means)
    return assemble(sec_ids, exchange(parcels), blocks_dev, comps)


def solution(mesh):
    placed = (
        P(("gx", "gy"), None, None),
        P(("gx", "gy"), None, None),
        P(("gx", "gy"), None, None),
        P(("gx", "gy"), None),
        P(("gx", "gy")),
        P(("gx", "gy")),
        P(("gx", "gy")),
    )
    return jax.shard_map(
        body, mesh=mesh, in_specs=placed, out_specs=P(("gx", "gy"), None, None), check_vma=False
    )
```

profile of v0, /device:TPU:0, one launch (start us, length us, event | category | flops | bytes accessed | tf_op | source)
XLA Modules:
  0.0 185.8 jit_solution(9809599998579340718)
XLA Ops:
  0.0 0.7 and_select_fusion.3
  1.1 0.7 and_select_fusion.1
  2.3 14.4 %all_to_all.39 = s32[32,2,16]{2,1,0:T(2,128)S(1)} all-to-all(s32[32,2,16]{2,1,0:T(2,128)S(1)} %copy.12), channel_id=1, replica_groups=mesh['gx'=4,'gy'=8] {'gx','gy'}, dimensions={0} | all-to-all | bytes 8192 | tf_op jit(solution)/shard_map/all_to_all | solution.py:26
  16.8 0.7 reshape_squeeze.7.ids
  17.4 4.3 %gather_rows.3 = f32[64,8,768]{2,1,0:T(8,128)} custom-call(s32[512]{0:T(512)} %reshape_squeeze.7.ids, f32[3,384,128]{2,1,0:T(8,128)} %bitcast.16, f32[3,384,128]{2,1,0:T(8,128)} %bitcast.18), custom_call_target="tpu_custom_call" | custom-call | tf_op jit(solution)/shard_map/gather_rows/pallas_call | solution.py:44
  21.8 2.8 %all-to-all-start.1 = ((f32[32,16,768]{2,1,0:T(8,128)}), f32[32,16,768]{2,1,0:T(8,128)S(1)}, u32[]{:S(2)}, u32[]{:S(2)}) async-start(f32[32,16,768]{2,1,0:T(8,128)} %bitcast.12), calls=%async_computation.1 | async-start | bytes 3145728 | tf_op jit(solution)/shard_map/all_to_all | solution.py:26
  26.2 0.8 constant_dynamic-update-slice_fusion.3
  27.7 0.9 fusion.1
  29.2 0.8 constant_dynamic-update-slice_fusion.feats
  30.0 2.7 %copy-done = bf16[256,48,256]{2,1,0:T(8,128)(2,1)} copy-done((bf16[256,48,256]{2,1,0:T(8,128)(2,1)}, bf16[256,48,256]{2,1,0:T(8,128)(2,1)S(1)}, u32[]{:S(2)}) %copy-start) | copy-done | bytes 6291480
  33.3 4.4 %gather_rows.2 = f32[64,8,768]{2,1,0:T(8,128)} custom-call(s32[512]{0:T(512)} %reshape_squeeze.6.ids, f32[3,384,128]{2,1,0:T(8,128)} %bitcast.17, f32[3,384,128]{2,1,0:T(8,128)} %bitcast.19), custom_call_target="tpu_custom_call" | custom-call | tf_op jit(solution)/shard_map/gather_rows/pallas_call | solution.py:44
  37.8 24.6 %all-to-all-done.1 = f32[32,16,768]{2,1,0:T(8,128)S(1)} async-done(((f32[32,16,768]{2,1,0:T(8,128)}), f32[32,16,768]{2,1,0:T(8,128)S(1)}, u32[]{:S(2)}, u32[]{:S(2)}) %all-to-all-start.1) | async-done | bytes 1572896 | tf_op jit(solution)/shard_map/all_to_all | solution.py:26
  62.4 3.6 %all-to-all-start.2 = ((f32[32,16,768]{2,1,0:T(8,128)}), f32[32,16,768]{2,1,0:T(8,128)S(1)}, u32[]{:S(2)}, u32[]{:S(2)}) async-start(f32[32,16,768]{2,1,0:T(8,128)} %bitcast.13), calls=%async_computation.2 | async-start | bytes 3145728 | tf_op jit(solution)/shard_map/all_to_all | solution.py:26
  66.0 0.8 fusion.4.weights
  66.8 18.5 %pri_means.1.means = f32[256,8,256]{2,1,0:T(8,128)} custom-call(s32[256]{0:T(256)} %copy-done.7, f32[512,768]{1,0:T(8,128)} %bitcast.11, bf16[256,48,256]{2,1,0:T(8,128)(2,1)} %copy-done), custom_call_target="tpu_custom_call" | custom-call | flops 1073741824 | bytes 8388608 | tf_op jit(solution)/shard_map/pri_means/pallas_call | solution.py:138
  85.3 18.3 %all-to-all-done.2 = f32[32,16,768]{2,1,0:T(8,128)S(1)} async-done(((f32[32,16,768]{2,1,0:T(8,128)}), f32[32,16,768]{2,1,0:T(8,128)S(1)}, u32[]{:S(2)}, u32[]{:S(2)}) %all-to-all-start.2) | async-done | bytes 1572896 | tf_op jit(solution)/shard_map/all_to_all | solution.py:26
  103.6 1.2 copy-done.2
  104.9 50.6 %coupling.1 = f32[512,3,128]{2,1,0:T(4,128)} custom-call(s32[256]{0:T(256)} %copy-done.6, f32[512,768]{1,0:T(8,128)} %bitcast.14, bf16[256,48,256]{2,1,0:T(8,128)(2,1)} %copy-done, f32[256,256]{1,0:T(8,128)} %fusion.4.weights, f32[256,8,256]{2,1,0:T(8,128)} %pri_means.1.means), custom_call_target="tpu_custom_call" | custom-call | flops 1073741824 | bytes 8388608 | tf_op jit(solution)/shard_map/coupling/pallas_call | solution.py:159
  155.4 2.3 %all_to_all.32 = f32[32,16,384]{2,1,0:T(8,128)} reshape(f32[512,3,128]{2,1,0:T(4,128)} %coupling.1) | data formatting | bytes 1572864 | tf_op jit(solution)/shard_map/all_to_all | solution.py:26
  157.8 3.8 %all-to-all-start.3 = ((f32[32,16,384]{2,1,0:T(8,128)}), f32[32,16,384]{2,1,0:T(8,128)S(1)}, u32[]{:S(2)}, u32[]{:S(2)}) async-start(f32[32,16,384]{2,1,0:T(8,128)} %all_to_all.32), calls=%async_computation.3 | async-start | bytes 1572864 | tf_op jit(solution)/shard_map/all_to_all | solution.py:26
  161.6 0.7 broadcast_in_dim_reshape_squeeze.3.ids
  162.2 19.9 %all-to-all-done.3 = f32[32,16,384]{2,1,0:T(8,128)S(1)} async-done(((f32[32,16,384]{2,1,0:T(8,128)}), f32[32,16,384]{2,1,0:T(8,128)S(1)}, u32[]{:S(2)}, u32[]{:S(2)}) %all-to-all-start.3) | async-done | bytes 786464 | tf_op jit(solution)/shard_map/all_to_all | solution.py:26
  182.2 0.9 copy-done.4
  183.0 2.7 %assemble.1 = f32[3,384,128]{2,1,0:T(8,128)} custom-call(s32[1,512]{1,0:T(1,128)} %broadcast_in_dim_reshape_squeeze.3.ids, f32[512,384]{1,0:T(8,128)} %bitcast.15), custom_call_target="tpu_custom_call" | custom-call | tf_op jit(solution)/shard_map/assemble/pallas_call | solution.py:195
  (37 shorter events, 4.5 us)
Async XLA Ops:
  0.9 20.9 %copy-start.6 = (s32[256]{0:T(256)}, s32[256]{0:T(256)S(1)}, u32[]{:S(2)}) copy-start(s32[256]{0:T(256)S(1)} %multiply_add_fusion.2.slots) | copy-start | bytes 3076
  2.0 19.8 %copy-start.7 = (s32[256]{0:T(256)}, s32[256]{0:T(256)S(1)}, u32[]{:S(2)}) copy-start(s32[256]{0:T(256)S(1)} %multiply_add_fusion.1.slots) | copy-start | bytes 3076
  21.8 2.9 %copy-start.3 = (f32[256,3,256]{2,0,1:T(8,128)S(1)}, f32[256,3,256]{2,0,1:T(8,128)}, u32[]{:S(2)}) copy-start(f32[256,3,256]{2,0,1:T(8,128)} %param.9) | copy-start | bytes 2359300
  21.8 40.6 %all-to-all-start.1 = ((f32[32,16,768]{2,1,0:T(8,128)}), f32[32,16,768]{2,1,0:T(8,128)S(1)}, u32[]{:S(2)}, u32[]{:S(2)}) async-start(f32[32,16,768]{2,1,0:T(8,128)} %bitcast.12), calls=%async_computation.1 | async-start | bytes 3145728 | tf_op jit(solution)/shard_map/all_to_all | solution.py:26
  30.0 2.7 %copy-start = (bf16[256,48,256]{2,1,0:T(8,128)(2,1)}, bf16[256,48,256]{2,1,0:T(8,128)(2,1)S(1)}, u32[]{:S(2)}) copy-start(bf16[256,48,256]{2,1,0:T(8,128)(2,1)S(1)} %constant_dynamic-update-slice_fusion.feats) | copy-start | bytes 18874372
  37.8 28.2 %copy-start.5 = (f32[256,256]{1,0:T(8,128)S(1)}, f32[256,256]{1,0:T(8,128)}, u32[]{:S(2)}) copy-start(f32[256,256]{1,0:T(8,128)} %param.10) | copy-start | bytes 786436
  37.8 28.2 %copy-start.8 = (s32[256]{0:T(256)S(1)}, s32[256]{0:T(256)}, u32[]{:S(2)}) copy-start(s32[256]{0:T(256)} %param.11) | copy-start | bytes 3076
  62.4 4.4 %copy-start.1 = (f32[32,16,768]{2,1,0:T(8,128)}, f32[32,16,768]{2,1,0:T(8,128)S(1)}, u32[]{:S(2)}) copy-start(f32[32,16,768]{2,1,0:T(8,128)S(1)} %all-to-all-done.1) | copy-start | bytes 4718596
  62.4 41.2 %all-to-all-start.2 = ((f32[32,16,768]{2,1,0:T(8,128)}), f32[32,16,768]{2,1,0:T(8,128)S(1)}, u32[]{:S(2)}, u32[]{:S(2)}) async-start(f32[32,16,768]{2,1,0:T(8,128)} %bitcast.13), calls=%async_computation.2 | async-start | bytes 3145728 | tf_op jit(solution)/shard_map/all_to_all | solution.py:26
  103.6 1.2 copy-start.2
  157.8 24.4 %all-to-all-start.3 = ((f32[32,16,384]{2,1,0:T(8,128)}), f32[32,16,384]{2,1,0:T(8,128)S(1)}, u32[]{:S(2)}, u32[]{:S(2)}) async-start(f32[32,16,384]{2,1,0:T(8,128)} %all_to_all.32), calls=%async_computation.3 | async-start | bytes 1572864 | tf_op jit(solution)/shard_map/all_to_all | solution.py:26
  182.2 0.9 copy-start.4
where the time goes:
time: 187 us; the launch traced here: 186 us
  Pallas kernels  80.6 us (43%)
  waiting for transfers between devices  62.9 us (34%)
  blocking collectives  14.4 us (8%)
  local copies, waits for them, and re-layouts  10.3 us (6%)
  starting transfers between devices  10.2 us (5%)
  other arithmetic  7.29 us (4%)
    all_to_all x3, waiting for transfers between devices, exchange(): lax.all_to_all(x, ('gx', 'gy'), split_axis=0, concat_axis=0, tiled=True)  62.9 us
    pallas_call x1, Pallas kernels, coupling(): pl.pallas_call(sec_kernel, grid_spec=pltpu.PrefetchScalarGridSpec(num_sca...  50.6 us
    pallas_call x1, Pallas kernels, pri_means(): pl.pallas_call(pri_kernel, grid_spec=pltpu.PrefetchScalarGridSpec(num_sca...  18.5 us
    all_to_all x1, blocking collectives, exchange(): lax.all_to_all(x, ('gx', 'gy'), split_axis=0, concat_axis=0, tiled=True)  14.4 us
    all_to_all x3, starting transfers between devices, exchange(): lax.all_to_all(x, ('gx', 'gy'), split_axis=0, concat_axis=0, tiled=True)  10.2 us
    pallas_call x2, Pallas kernels, gather_rows(): pl.pallas_call(gather_kernel, out_shape=jax.ShapeDtypeStruct((rows // UNR...  8.79 us
    unnamed x19, local copies, waits for them, and re-layouts  5.33 us
  transfers between devices with their start and end apart: 3, of which 3 were waited for; matrix products, arithmetic and copies ran while one was open for 4% of the time, Pallas kernels for 12%

commit v1 on v0

v1 whole, which is shorter than its diff:
```python
import functools
import jax
import jax.numpy as jnp
from jax import lax
from jax.experimental import pallas as pl
from jax.experimental.pallas import tpu as pltpu
from jax.sharding import PartitionSpec as P

GROUP = 16
CHUNKS = 2
F32, BF16 = jnp.float32, jnp.bfloat16
MESH = pl.DeviceIdType.MESH


def ranks_of(owners):
    positions = jnp.arange(owners.shape[0], dtype=jnp.int32)
    same = (owners[:, None] == owners[None, :]) & (positions[:, None] > positions[None, :])
    return jnp.sum(same.astype(jnp.int32), axis=1)


def pick(values, where, size, empty):
    match = where[:, None] == jnp.arange(size, dtype=jnp.int32)[None, :]
    return jnp.sum(jnp.where(match, (values - empty)[:, None], 0), axis=0) + empty


def exchange(x):
    return lax.all_to_all(x, ("gx", "gy"), split_axis=0, concat_axis=0, tiled=True)


def rounded(x):
    return x.astype(BF16).astype(F32)


def stack_rows(rows, iota):
    out = jnp.zeros(iota.shape, F32)
    for i, row in rows:
        out = jnp.where(iota == i, row, out)
    return out


def disp_rows(row, n):
    iota = lax.broadcasted_iota(jnp.int32, (8, n), 0)
    u = [row[:, (3 + c) * n : (4 + c) * n] for c in range(3)]
    full = stack_rows([(i + 4 * h, u[i]) for h in range(2) for i in range(3)], iota)
    full = jnp.where((iota == 3) | (iota == 7), 1.0, full)
    both = jnp.where(iota < 4, rounded(full), full - rounded(full)).astype(BF16)
    return jnp.concatenate([both, both], axis=1)


def split_three(full):
    high = rounded(full)
    rest = full - high
    mid = rounded(rest)
    return high, mid, rest - mid


def point_features(qp, s):
    iota = lax.broadcasted_iota(jnp.int32, (8, qp.shape[2]), 0)
    x = [qp[c, pl.ds(s, 1), :] for c in range(3)]
    square = 1.0 + 2.0 * (x[0] * x[0] + x[1] * x[1] + x[2] * x[2])
    full = stack_rows([(0, x[0]), (1, x[1]), (2, x[2]), (3, 1.0), (4, square)], iota)
    high, mid, low = split_three(full)
    return jnp.concatenate([high, mid, high, low, high, mid], axis=0).astype(BF16)


def kernel_values(row, feat, n):
    iota = lax.broadcasted_iota(jnp.int32, (8, n), 0)
    x = [row[:, c * n : (c + 1) * n] for c in range(3)]
    square = 2.0 * (x[0] * x[0] + x[1] * x[1] + x[2] * x[2])
    full = stack_rows(
        [(0, -4.0 * x[0]), (1, -4.0 * x[1]), (2, -4.0 * x[2]), (3, square), (4, 1.0)], iota
    )
    high, mid, low = split_three(full)
    left = jnp.concatenate([high, high, mid, high, low, mid], axis=0)
    kern = 1.0 / jnp.dot(left.T.astype(BF16), feat, preferred_element_type=F32)
    kh = kern.astype(BF16)
    return kh, (kern - kh.astype(F32)).astype(BF16)


def fused_kernel(
    pri_ids, sec_ids, pri_slots, sec_slots, order, inverse, counts,
    hot_ids, coords, disp, qp, weights, gap,
    pri_send, pri_recv, sec_send, means, parcels, both_s, gap_s, *rest,
):
    chunks = sec_send.shape[0]
    sec_recv, rest = rest[:chunks], rest[chunks:]
    par_send, rest = rest[:chunks], rest[chunks:]
    par_recv, rest = rest[:chunks], rest[chunks:]
    send_sem, recv_sem = rest
    ny = lax.axis_size("gy")
    devices, cap, width = pri_send.shape
    cap_c = sec_send.shape[2]
    n = width // 6
    segs = means.shape[0]
    points = qp.shape[2]
    me = lax.axis_index("gx") * ny + lax.axis_index("gy")

    def partner(t):
        return lax.rem(me + t, devices)

    def place(p):
        return (p // ny, lax.rem(p, ny))

    def copy(src, dst, k, t):
        p = partner(t)
        return pltpu.make_async_remote_copy(
            src_ref=src.at[p],
            dst_ref=dst.at[me],
            send_sem=send_sem.at[k, t],
            recv_sem=recv_sem.at[k, t],
            device_id=place(p),
            device_id_type=MESH,
        )

    half = devices // 2

    def far_first(i):
        t = i + half
        return jnp.where(t >= devices, t - devices + 1, t)

    def start_all(src, dst, k):
        @pl.loop(0, devices - 1)
        def _(i):
            copy(src, dst, k, far_first(i)).start()

    def wait_recv(src, dst, k):
        @pl.loop(1, devices)
        def _(t):
            copy(src, dst, k, t).wait_recv()

    def wait_send(src, dst, k):
        @pl.loop(1, devices)
        def _(t):
            copy(src, dst, k, t).wait_send()

    def gather(ids, base, dst, p, rows):
        for j in range(rows):
            b = ids[base + j]
            for c in range(3):
                dst[p, j : j + 1, c * n : (c + 1) * n] = coords[c, pl.ds(b, 1), :]
                k = 3 + c
                dst[p, j : j + 1, k * n : (k + 1) * n] = disp[c, pl.ds(b, 1), :]

    def lift(i, c, dst, p):
        base = (c * devices + p) * cap_c
        for j in range(cap_c):
            k = inverse[base + j]
            for d in range(3):
                dst[p, j : j + 1, d * n : (d + 1) * n] = parcels[k, d : d + 1, :]

    barrier = pltpu.get_barrier_semaphore()

    @pl.loop(1, devices)
    def _(t):
        pl.semaphore_signal(barrier, inc=1, device_id=place(partner(t)), device_id_type=MESH)

    @pl.loop(0, devices - 1)
    def _(i):
        p = partner(far_first(i))
        gather(pri_ids, p * cap, pri_send, p, cap)

    gather(pri_ids, me * cap, pri_recv, me, cap)
    pl.semaphore_wait(barrier, devices - 1)
    start_all(pri_send, pri_recv, 0)
    for c in range(chunks):

        @pl.loop(0, devices - 1)
        def _(i):
            p = partner(far_first(i))
            gather(sec_ids, (c * devices + p) * cap_c, sec_send.at[c], p, cap_c)

        gather(sec_ids, (c * devices + me) * cap_c, sec_recv[c], me, cap_c)
        start_all(sec_send.at[c], sec_recv[c], 1 + c)

    def group_values(nodes, slot_of, seg_of):
        for g in range(GROUP):
            slot = slot_of(g)
            row = nodes[slot // nodes.shape[1], pl.ds(lax.rem(slot, nodes.shape[1]), 1), :]
            kh, kl = kernel_values(row, point_features(qp, seg_of(g)), n)
            both_s[g, :n] = kh
            both_s[g, n:] = kl

    def group_mean(nodes, slot):
        row = nodes[slot // nodes.shape[1], pl.ds(lax.rem(slot, nodes.shape[1]), 1), :]
        return disp_rows(row, n)

    def mean_of(lhs, g):
        a = jnp.dot(lhs, both_s[g], preferred_element_type=F32)
        total = a + pltpu.roll(a, 4, 0)
        inv = 1.0 / total[3:4]
        return total * inv, inv

    wait_recv(pri_send, pri_recv, 0)

    @pl.loop(0, segs // GROUP)
    def _(i):
        group_values(pri_recv, lambda g: pri_slots[i * GROUP + g], lambda g: i * GROUP + g)
        for g in range(GROUP):
            s = i * GROUP + g
            means[s] = mean_of(group_mean(pri_recv, pri_slots[s]), g)[0]

    parcels[segs] = jnp.zeros(parcels.shape[1:], F32)
    iota = lax.broadcasted_iota(jnp.int32, (8, points), 0)
    lane = lax.broadcasted_iota(jnp.int32, (1, points), 1)
    steps = segs // chunks // GROUP
    for c in range(chunks):
        nodes = sec_recv[c]
        wait_recv(sec_send.at[c], nodes, 1 + c)

        @pl.loop(c * steps, (c + 1) * steps)
        def _(i):
            group_values(nodes, lambda g: sec_slots[i * GROUP + g], lambda g: order[i * GROUP + g])
            for g in range(GROUP):
                s = order[i * GROUP + g]
                mean, inv = mean_of(group_mean(nodes, sec_slots[i * GROUP + g]), g)
                w = jnp.where(lane < counts[s], weights[pl.ds(s, 1), :], 0.0)
                diff = (mean - means[s]) * (w * inv)
                high = rounded(diff)
                gap_s[g] = jnp.where(iota < 4, high, diff - high)
            for g in range(GROUP):
                y = lax.dot_general(
                    gap_s[g].astype(BF16), both_s[g], (((1,), (1,)), ((), ())),
                    preferred_element_type=F32,
                )
                y = y[:, :n] + y[:, n:]
                parcels[i * GROUP + g] = y + pltpu.roll(y, 4, 0)

        @pl.loop(0, devices - 1)
        def _(i):
            lift(i, c, par_send[c], partner(far_first(i)))

        lift(0, c, par_recv[c], me)
        start_all(par_send[c], par_recv[c], 1 + chunks + c)

    wait_send(pri_send, pri_recv, 0)
    for c in range(chunks):
        wait_send(sec_send.at[c], sec_recv[c], 1 + c)
    blocks = gap.shape[1]
    slots_c = devices * cap_c
    for c in range(chunks):
        wait_recv(par_send[c], par_recv[c], 1 + chunks + c)
        match = lax.broadcasted_iota(jnp.int32, (blocks, slots_c), 0) == hot_ids[c : c + 1]
        select = jnp.where(match, 1.0, 0.0).astype(BF16)
        for d in range(3):
            x = par_recv[c][:, :, d * n : (d + 1) * n].reshape(slots_c, n)
            high, mid, low = split_three(x)
            pieces = jnp.concatenate([high, mid, low], axis=1).astype(BF16)
            y = jnp.dot(select, pieces, preferred_element_type=F32)
            y = y[:, :n] + (y[:, n : 2 * n] + y[:, 2 * n :])
            gap[d] = y if c == 0 else gap[d] + y
    for c in range(chunks):
        wait_send(par_send[c], par_recv[c], 1 + chunks + c)


def fused(tables, hot_ids, coords, disp, qp, weights, devices, cap, chunks):
    comps, blocks, n = coords.shape
    _, segs, points = qp.shape
    cap_c = cap // chunks
    width = 2 * comps * n
    vmem, smem = pl.BlockSpec(memory_space=pltpu.VMEM), pl.BlockSpec(memory_space=pltpu.SMEM)
    nodes_c = [pltpu.VMEM((devices, cap_c, width), F32) for _ in range(chunks)]
    parts_c = [pltpu.VMEM((devices, cap_c, comps * n), F32) for _ in range(2 * chunks)]
    kinds = 1 + 2 * chunks
    return pl.pallas_call(
        fused_kernel,
        out_shape=jax.ShapeDtypeStruct((comps, blocks, n), F32),
        in_specs=[smem] * len(tables) + [vmem] * 5,
        out_specs=vmem,
        scratch_shapes=[
            pltpu.VMEM((devices, cap, width), F32),
            pltpu.VMEM((devices, cap, width), F32),
            pltpu.VMEM((chunks, devices, cap_c, width), F32),
            pltpu.VMEM((segs, 8, points), F32),
            pltpu.VMEM((segs + 1, 8, n), F32),
            pltpu.VMEM((GROUP, 2 * n, points), BF16),
            pltpu.VMEM((GROUP, 8, points), F32),
            *nodes_c,
            *parts_c,
            pltpu.SemaphoreType.DMA((kinds, devices)),
            pltpu.SemaphoreType.DMA((kinds, devices)),
        ],
        compiler_params=pltpu.CompilerParams(collective_id=0, has_side_effects=True),
        name="fused",
    )(*tables, hot_ids, coords, disp, qp, weights)


def body(node_coords, node_disp, qpoints, qweights, qcount, sec_block, pri_block):
    devices = lax.axis_size("gx") * lax.axis_size("gy")
    blocks = node_coords.shape[0]
    segs = qpoints.shape[0]
    cap = 2 * segs // devices
    chunks = CHUNKS
    cap_c = cap // chunks
    slots, slots_c = devices * cap, devices * cap_c
    pri_owner, sec_owner = pri_block // blocks, sec_block // blocks
    pri_slot = pri_owner * cap + ranks_of(pri_owner)
    pri_request = pick(pri_block % blocks, pri_slot, slots, 0)
    rank = ranks_of(sec_owner)
    start = jnp.sum((sec_owner[:, None] > sec_owner[None, :]).astype(jnp.int32), axis=1)
    position = start + rank
    chunk = position % chunks
    turn = chunk * (segs // chunks) + position // chunks
    slot_c = sec_owner * cap_c + rank // chunks
    place = chunk * slots_c + slot_c
    sec_request = pick(sec_block % blocks, place, slots, 0)
    inverse = pick(turn, place, slots, segs)
    order = pick(jnp.arange(segs, dtype=jnp.int32), turn, segs, 0)
    sec_slot = pick(slot_c, turn, segs, 0)
    sec_rows = sec_request.reshape(chunks, devices, cap_c).transpose(1, 0, 2)
    requests = jnp.stack([pri_request.reshape(devices, cap), sec_rows.reshape(devices, cap)], axis=1)
    received = exchange(requests)
    pri_ids = received[:, 0].reshape(slots)
    sec_ids = received[:, 1].reshape(devices, chunks, cap_c).transpose(1, 0, 2).reshape(slots)
    tables = (pri_ids, sec_ids, pri_slot, sec_slot, order, inverse, qcount)
    gap = fused(
        tables,
        sec_ids.reshape(chunks, slots_c),
        node_coords.transpose(1, 0, 2),
        node_disp.transpose(1, 0, 2),
        qpoints.transpose(1, 0, 2),
        qweights,
        devices,
        cap,
        chunks,
    )
    return gap.transpose(1, 0, 2)


def solution(mesh):
    placed = (
        P(("gx", "gy"), None, None),
        P(("gx", "gy"), None, None),
        P(("gx", "gy"), None, None),
        P(("gx", "gy"), None),
        P(("gx", "gy")),
        P(("gx", "gy")),
        P(("gx", "gy")),
    )
    return jax.shard_map(
        body, mesh=mesh, in_specs=placed, out_specs=P(("gx", "gy"), None, None), check_vma=False
    )
```

time: 187 us -> 132 us (0.71)
  waiting for transfers between devices: 62.9 us -> 5.95 us
  Pallas kernels: 80.6 us -> 109 us
  blocking collectives: 14.4 us -> 0 us
  other arithmetic: 7.29 us -> 2.78 us
  local copies, waits for them, and re-layouts: 10.3 us -> 5.99 us
  starting transfers between devices: 10.2 us -> 7.33 us
    all_to_all x3 -> x1, waiting for transfers between devices: 62.9 us -> 5.95 us  [exchange(): lax.all_to_all(x, ('gx', 'gy'), split_axis=0, concat_axis=0, tiled=True)]
    pallas_call x5 -> x1, Pallas kernels: 80.6 us -> 109 us  [fused(): pl.pallas_call(fused_kernel, out_shape=jax.ShapeDtypeStruct((comps, block...]
    all_to_all x1 -> x0, blocking collectives: 14.4 us -> none  [exchange(): lax.all_to_all(x, ('gx', 'gy'), split_axis=0, concat_axis=0, tiled=True)]
    unnamed x5 -> x0, other arithmetic: 3.55 us -> none
    all_to_all x3 -> x1, starting transfers between devices: 10.2 us -> 7.33 us  [exchange(): lax.all_to_all(x, ('gx', 'gy'), split_axis=0, concat_axis=0, tiled=True)]
    unnamed x19 -> x6, local copies, waits for them, and re-layouts: 5.33 us -> 2.87 us
    all_to_all x1 -> x0, local copies, waits for them, and re-layouts: 2.33 us -> none  [exchange(): lax.all_to_all(x, ('gx', 'gy'), split_axis=0, concat_axis=0, tiled=True)]
  transfers between devices with their start and end apart: 3 -> 1, of which waited for: 3 -> 1; matrix products, arithmetic and copies ran while one was open for 4% -> 1% of each run, Pallas kernels for 12% -> 0%
where the time goes in v1:
time: 132 us; the launch traced here: 131 us
  Pallas kernels  109 us (83%)
  starting transfers between devices  7.33 us (6%)
  local copies, waits for them, and re-layouts  5.99 us (5%)
  waiting for transfers between devices  5.95 us (5%)
  other arithmetic  2.78 us (2%)
    pallas_call x1, Pallas kernels, fused(): pl.pallas_call(fused_kernel, out_shape=jax.ShapeDtypeStruct((comps, block...  109 us
    all_to_all x1, starting transfers between devices, exchange(): lax.all_to_all(x, ('gx', 'gy'), split_axis=0, concat_axis=0, tiled=True)  7.33 us
    all_to_all x1, waiting for transfers between devices, exchange(): lax.all_to_all(x, ('gx', 'gy'), split_axis=0, concat_axis=0, tiled=True)  5.95 us
    unnamed x6, local copies, waits for them, and re-layouts  2.87 us
  transfers between devices with their start and end apart: 1, of which 1 were waited for; matrix products, arithmetic and copies ran while one was open for 1% of the time, Pallas kernels for 0%

profile of v1, /device:TPU:0, one launch (start us, length us, event | category | flops | bytes accessed | tf_op | source)
XLA Modules:
  0.0 131.5 jit_solution(4628814039016283245)
XLA Ops:
  0.0 0.7 and_select_fusion.1
  0.7 0.2 convert_reduce_fusion.1
  0.9 0.4 copy-done.1
  1.4 0.2 convert_reduce_fusion.2
  1.6 0.1 select_reduce_fusion.2
  1.7 0.4 copy-done
  2.2 0.1 stack_reshape.6
  2.3 0.2 select_reduce_fusion
  2.5 0.1 reshape.53
  2.6 0.1 copy.19
  2.6 0.1 copy.20
  2.7 0.6 copy.21
  3.4 7.3 %all-to-all-start = ((s32[32,2,16]{2,1,0:T(2,128)}), s32[32,2,16]{2,1,0:T(2,128)S(1)}, u32[]{:S(2)}, u32[]{:S(2)}) async-start(s32[32,2,16]{2,1,0:T(2,128)} %copy.21), calls=%async_computation | async-start | bytes 65536 | tf_op jit(solution)/shard_map/all_to_all | solution.py:27
  10.7 0.6 broadcast_add_fusion.inverse
  11.3 0.7 select_reduce_fusion.3
  12.0 5.9 %all-to-all-done = s32[32,2,16]{2,1,0:T(2,128)S(1)} async-done(((s32[32,2,16]{2,1,0:T(2,128)}), s32[32,2,16]{2,1,0:T(2,128)S(1)}, u32[]{:S(2)}, u32[]{:S(2)}) %all-to-all-start) | async-done | bytes 4128 | tf_op jit(solution)/shard_map/all_to_all | solution.py:27
  17.9 0.1 fusion.6
  18.0 0.1 copy.25
  18.1 0.1 copy.23
  18.2 0.7 reshape_reshape.3.hot_ids
  18.8 0.7 reshape.54.sec_ids
  19.5 0.7 reshape_squeeze.6.pri_ids
  20.2 109.4 %fused.1 = f32[3,384,128]{2,1,0:T(8,128)} custom-call(s32[512]{0:T(512)} %reshape_squeeze.6.pri_ids, s32[512]{0:T(512)} %reshape.54.sec_ids, s32[256]{0:T(256)} %copy-done, s32[256]{0:T(256)} %get-tuple-element.8.sec_slots, s32[256]{0:T(256)} %get-tuple-element.7.order, s32[512]{0:T(512)} %broadcast_add_fusion.inverse, s32[256]{0:T(256)} %counts.1, ...), custom_call_target="tpu_custom_call" | custom-call | tf_op jit(solution)/shard_map/fused/pallas_call | solution.py:264
  129.6 1.9 %copy.27 = f32[384,3,128]{2,0,1:T(8,128)} copy(f32[384,3,128]{2,0,1:T(8,128)} %bitcast.9) | data formatting | bytes 1179648
  (6 shorter events, 0.0 us)
Async XLA Ops:
  0.7 0.7 copy-start.1
  1.6 0.6 copy-start
  3.4 14.6 %all-to-all-start = ((s32[32,2,16]{2,1,0:T(2,128)}), s32[32,2,16]{2,1,0:T(2,128)S(1)}, u32[]{:S(2)}, u32[]{:S(2)}) async-start(s32[32,2,16]{2,1,0:T(2,128)} %copy.21), calls=%async_computation | async-start | bytes 65536 | tf_op jit(solution)/shard_map/all_to_all | solution.py:27

commit v2 on v1

v2 whole, which is shorter than its diff:
```python
import functools
import jax
import jax.numpy as jnp
from jax import lax
from jax.experimental import pallas as pl
from jax.experimental.pallas import tpu as pltpu
from jax.sharding import PartitionSpec as P

GROUP = 16
PHASES = (2, 1, 1)
F32, BF16 = jnp.float32, jnp.bfloat16
MESH = pl.DeviceIdType.MESH


def rounded(x):
    return x.astype(BF16).astype(F32)


def stack_rows(rows, iota):
    out = jnp.zeros(iota.shape, F32)
    for i, row in rows:
        out = jnp.where(iota == i, row, out)
    return out


def disp_rows(row, n):
    iota = lax.broadcasted_iota(jnp.int32, (8, n), 0)
    u = [row[:, (3 + c) * n : (4 + c) * n] for c in range(3)]
    full = stack_rows([(i + 4 * h, u[i]) for h in range(2) for i in range(3)], iota)
    full = jnp.where((iota == 3) | (iota == 7), 1.0, full)
    both = jnp.where(iota < 4, rounded(full), full - rounded(full)).astype(BF16)
    return jnp.concatenate([both, both], axis=1)


def split_three(full):
    high = rounded(full)
    rest = full - high
    mid = rounded(rest)
    return high, mid, rest - mid


def point_features(qp, s):
    iota = lax.broadcasted_iota(jnp.int32, (8, qp.shape[2]), 0)
    x = [qp[c, pl.ds(s, 1), :] for c in range(3)]
    square = 1.0 + 2.0 * (x[0] * x[0] + x[1] * x[1] + x[2] * x[2])
    full = stack_rows([(0, x[0]), (1, x[1]), (2, x[2]), (3, 1.0), (4, square)], iota)
    high, mid, low = split_three(full)
    return jnp.concatenate([high, mid, high, low, high, mid], axis=0).astype(BF16)


def kernel_values(row, feat, n):
    iota = lax.broadcasted_iota(jnp.int32, (8, n), 0)
    x = [row[:, c * n : (c + 1) * n] for c in range(3)]
    square = 2.0 * (x[0] * x[0] + x[1] * x[1] + x[2] * x[2])
    full = stack_rows(
        [(0, -4.0 * x[0]), (1, -4.0 * x[1]), (2, -4.0 * x[2]), (3, square), (4, 1.0)], iota
    )
    high, mid, low = split_three(full)
    left = jnp.concatenate([high, high, mid, high, low, mid], axis=0)
    kern = 1.0 / jnp.dot(left.T.astype(BF16), feat, preferred_element_type=F32)
    kh = kern.astype(BF16)
    return kh, (kern - kh.astype(F32)).astype(BF16)


def floor_div(x, m):
    return jnp.floor((x + 0.5) * (1.0 / m))


def whole(x, size):
    return jnp.clip(x.astype(jnp.int32), 0, size - 1)


def one_hot_sum(lhs, match):
    return lax.dot_general(
        lhs.astype(BF16), jnp.where(match, 1.0, 0.0).astype(BF16), (((1,), (1,)), ((), ())),
        preferred_element_type=F32,
    )


def sixteens(x):
    high = jnp.floor(x * 0.0625)
    return high, x - 16.0 * high


def owners_of(block, blocks, cap):
    segs = block.shape[1]
    owner = floor_div(block, blocks)
    across = jnp.broadcast_to(owner, (segs, segs))
    down = across.T
    before = lax.broadcasted_iota(jnp.int32, (segs, segs), 0) < lax.broadcasted_iota(
        jnp.int32, (segs, segs), 1
    )
    same = jnp.where((down == across) & before, 1.0, 0.0)
    rank = jnp.sum(same, axis=0, keepdims=True)
    start = jnp.sum(jnp.where(down < across, 1.0, 0.0), axis=0, keepdims=True)
    return owner, block - owner * blocks, rank, start


def deal(owner, rank, start, segs, devices, cap):
    total = sum(PHASES)
    quarter = cap // total
    position = start + rank
    phase = position - total * floor_div(position, total)
    turn = place = slot = lane = jnp.zeros_like(owner)
    first = 0
    for count in PHASES:

        def before(x):
            turns = floor_div(x, total)
            return turns * count + jnp.clip(x - total * turns - first, 0.0, count)

        inside = (phase >= first) & (phase < first + count)
        spot = before(position)
        nth = spot - before(start)
        here = owner * (count * quarter) + nth
        turn = jnp.where(inside, spot + first * (segs // total), turn)
        slot = jnp.where(inside, here, slot)
        place = jnp.where(inside, here + first * quarter * devices, place)
        lane = jnp.where(inside, nth + (cap + first * quarter), lane)
        first += count
    return turn, slot, place, lane


def fused_kernel(
    pri_block, sec_block, counts, coords, disp, qp, weights, gap,
    req_send, req_recv, req_rows, ids, table_v, table, hot,
    pri_send, pri_recv, means, parcels, both_s, gap_s, *rest,
):
    chunks = len(PHASES)
    sec_send, rest = rest[:chunks], rest[chunks:]
    sec_recv, rest = rest[:chunks], rest[chunks:]
    par_send, rest = rest[:chunks], rest[chunks:]
    par_recv, rest = rest[:chunks], rest[chunks:]
    send_sem, recv_sem, local_sem = rest
    ny = lax.axis_size("gy")
    devices, cap, width = pri_send.shape
    n = width // 6
    segs, points = weights.shape
    blocks = coords.shape[1]
    slots = devices * cap
    total = sum(PHASES)
    quarter = cap // total
    firsts = [sum(PHASES[:c]) for c in range(chunks)]
    caps = [m * quarter for m in PHASES]
    me = lax.axis_index("gx") * ny + lax.axis_index("gy")

    def partner(t):
        return lax.rem(me + t, devices)

    def device(p):
        return (p // ny, lax.rem(p, ny))

    def copy(src, dst, k, t):
        p = partner(t)
        return pltpu.make_async_remote_copy(
            src_ref=src.at[p],
            dst_ref=dst.at[me],
            send_sem=send_sem.at[k, t],
            recv_sem=recv_sem.at[k, t],
            device_id=device(p),
            device_id_type=MESH,
        )

    half = devices // 2

    def far_first(i):
        t = i + half
        return jnp.where(t >= devices, t - devices + 1, t)

    def fill_and_start(fill, src, dst, k):
        fill(partner(far_first(0)), src)

        @pl.loop(1, devices - 1)
        def _(i):
            fill(partner(far_first(i)), src)
            copy(src, dst, k, far_first(i - 1)).start()

        fill(me, dst)
        copy(src, dst, k, far_first(devices - 2)).start()

    def wait_recv(src, dst, k):
        @pl.loop(1, devices)
        def _(t):
            copy(src, dst, k, t).wait_recv()

    def wait_send(src, dst, k):
        @pl.loop(1, devices)
        def _(t):
            copy(src, dst, k, t).wait_send()

    barrier = pltpu.get_barrier_semaphore()

    @pl.loop(1, devices)
    def _(t):
        pl.semaphore_signal(barrier, inc=1, device_id=device(partner(t)), device_id_type=MESH)

    pri = pri_block[...].reshape(1, segs).astype(F32)
    sec = sec_block[...].reshape(1, segs).astype(F32)
    pri_owner, pri_local, pri_rank, _ = owners_of(pri, blocks, cap)
    sec_owner, sec_local, sec_rank, sec_start = owners_of(sec, blocks, cap)
    turn, slot, place, lane = deal(sec_owner, sec_rank, sec_start, segs, devices, cap)
    owner = jnp.concatenate([pri_owner, sec_owner], axis=1)
    column = jnp.concatenate([pri_rank, lane], axis=1)
    local = jnp.concatenate([pri_local, sec_local], axis=1)
    to_owner = lax.broadcasted_iota(jnp.int32, (devices, 2 * segs), 0).astype(F32) == owner
    to_owner = jnp.where(to_owner, 1.0, 0.0)
    at_lane = lax.broadcasted_iota(jnp.int32, (128, 2 * segs), 0).astype(F32) == column
    pieces = [
        lax.dot_general(
            to_owner.astype(BF16), jnp.where(at_lane, part, 0.0).astype(BF16),
            (((1,), (1,)), ((), ())), preferred_element_type=F32,
        )
        for part in sixteens(local)
    ]
    req_rows[...] = 16.0 * pieces[0] + pieces[1]

    @pl.loop(0, devices)
    def _(p):
        req_send[p] = whole(req_rows[pl.ds(p, 1), :], blocks)

    req_recv[me] = whole(req_rows[pl.ds(me, 1), :], blocks)
    pl.semaphore_wait(barrier, devices - 1)

    @pl.loop(0, devices - 1)
    def _(i):
        copy(req_send, req_recv, 0, far_first(i)).start()

    number = lax.broadcasted_iota(jnp.int32, (1, segs), 1).astype(F32)
    zero = jnp.zeros((4, segs), F32)
    rows = jnp.concatenate([*sixteens(number), *sixteens(slot), zero], axis=0)
    match = lax.broadcasted_iota(jnp.int32, (segs, segs), 0).astype(F32) == turn
    found = one_hot_sum(rows, match)
    rows = jnp.concatenate([*sixteens(turn + 1.0), zero, zero[:2]], axis=0)
    match = lax.broadcasted_iota(jnp.int32, (slots, segs), 0).astype(F32) == place
    inverse = one_hot_sum(rows, match)
    inverse = 16.0 * inverse[0:1] + inverse[1:2] - 1.0
    inverse = jnp.where(inverse < 0.0, float(segs), inverse)
    turns = lax.broadcasted_iota(jnp.int32, (1, segs), 1)
    sizes = jnp.zeros_like(turns)
    for c in range(chunks):
        sizes = jnp.where(turns >= firsts[c] * (segs // total), devices * caps[c], sizes)
    table_v[0:1, :segs] = whole(pri_owner * cap + pri_rank, slots)
    table_v[1:2, :segs] = whole(16.0 * found[0:1] + found[1:2], segs)
    table_v[2:3, :segs] = whole(16.0 * found[2:3] + found[3:4], sizes)
    table_v[3:4, :] = whole(inverse, segs + 1)
    load_table = pltpu.make_async_copy(table_v, table, local_sem.at[0])
    load_table.start()

    wait_recv(req_send, req_recv, 0)
    load_ids = pltpu.make_async_copy(req_recv, ids, local_sem.at[1])
    load_ids.start()
    load_table.wait()
    load_ids.wait()

    def gather(base, count, p, dst):
        for j in range(count):
            b = ids[p, 0, base + j]
            for c in range(3):
                dst[p, j : j + 1, c * n : (c + 1) * n] = coords[c, pl.ds(b, 1), :]
                k = 3 + c
                dst[p, j : j + 1, k * n : (k + 1) * n] = disp[c, pl.ds(b, 1), :]

    fill_and_start(functools.partial(gather, 0, cap), pri_send, pri_recv, 1)
    for c in range(chunks):
        fill = functools.partial(gather, cap + firsts[c] * quarter, caps[c])
        fill_and_start(fill, sec_send[c], sec_recv[c], 2 + c)

    @pl.loop(0, devices)
    def _(p):
        req_rows[pl.ds(p, 1), :] = req_recv[p].astype(F32)

    high, low = sixteens(req_rows[...])
    for c in range(chunks):
        size = devices * caps[c]
        k = lax.broadcasted_iota(jnp.int32, (1, size), 1).astype(F32)
        from_row = floor_div(k, caps[c])
        from_lane = k - from_row * caps[c] + float(cap + firsts[c] * quarter)
        spread = lax.broadcasted_iota(jnp.int32, (128, size), 0).astype(F32) == from_lane
        spread = jnp.where(spread, 1.0, 0.0).astype(BF16)
        y = 16.0 * jnp.dot(high.astype(BF16), spread, preferred_element_type=F32)
        y = y + jnp.dot(low.astype(BF16), spread, preferred_element_type=F32)
        mine = lax.broadcasted_iota(jnp.int32, (devices, size), 0).astype(F32) == from_row
        hot[c : c + 1, :size] = jnp.sum(jnp.where(mine, y, 0.0), axis=0, keepdims=True)

    def row_of(nodes, spot):
        return nodes[spot // nodes.shape[1], pl.ds(lax.rem(spot, nodes.shape[1]), 1), :]

    def group_values(nodes, slot_of, seg_of):
        for g in range(GROUP):
            kh, kl = kernel_values(row_of(nodes, slot_of(g)), point_features(qp, seg_of(g)), n)
            both_s[g, :n] = kh
            both_s[g, n:] = kl

    def mean_of(row, g):
        a = jnp.dot(disp_rows(row, n), both_s[g], preferred_element_type=F32)
        sums = a + pltpu.roll(a, 4, 0)
        inv = 1.0 / sums[3:4]
        return sums * inv, inv

    wait_recv(pri_send, pri_recv, 1)

    @pl.loop(0, segs // GROUP)
    def _(i):
        group_values(pri_recv, lambda g: table[0, i * GROUP + g], lambda g: i * GROUP + g)
        for g in range(GROUP):
            s = i * GROUP + g
            means[s] = mean_of(row_of(pri_recv, table[0, s]), g)[0]

    parcels[segs] = jnp.zeros(parcels.shape[1:], F32)
    iota = lax.broadcasted_iota(jnp.int32, (8, points), 0)
    lanes = lax.broadcasted_iota(jnp.int32, (1, points), 1)
    steps = segs // total // GROUP
    for c in range(chunks):
        nodes = sec_recv[c]
        wait_recv(sec_send[c], nodes, 2 + c)

        @pl.loop(firsts[c] * steps, (firsts[c] + PHASES[c]) * steps)
        def _(i):
            group_values(nodes, lambda g: table[2, i * GROUP + g], lambda g: table[1, i * GROUP + g])
            for g in range(GROUP):
                s = table[1, i * GROUP + g]
                mean, inv = mean_of(row_of(nodes, table[2, i * GROUP + g]), g)
                w = jnp.where(lanes < counts[s], weights[pl.ds(s, 1), :], 0.0)
                diff = (mean - means[s]) * (w * inv)
                top = rounded(diff)
                gap_s[g] = jnp.where(iota < 4, top, diff - top)
            for g in range(GROUP):
                y = lax.dot_general(
                    gap_s[g].astype(BF16), both_s[g], (((1,), (1,)), ((), ())),
                    preferred_element_type=F32,
                )
                y = y[:, :n] + y[:, n:]
                parcels[i * GROUP + g] = y + pltpu.roll(y, 4, 0)

        def lift(p, dst):
            base = firsts[c] * quarter * devices + p * caps[c]
            for j in range(caps[c]):
                k = table[3, base + j]
                for d in range(3):
                    dst[p, d, j : j + 1, :] = parcels[k, d : d + 1, :]

        fill_and_start(lift, par_send[c], par_recv[c], 2 + chunks + c)

    wait_send(req_send, req_recv, 0)
    wait_send(pri_send, pri_recv, 1)
    for c in range(chunks):
        wait_send(sec_send[c], sec_recv[c], 2 + c)
    for c in range(chunks):
        wait_recv(par_send[c], par_recv[c], 2 + chunks + c)
        size = devices * caps[c]
        row = lax.broadcasted_iota(jnp.int32, (blocks, size), 0).astype(F32)
        select = jnp.where(row == hot[c : c + 1, :size], 1.0, 0.0).astype(BF16)
        for d in range(3):
            x = par_recv[c][:, d].reshape(size, n)
            top, mid, low = split_three(x)
            parts = jnp.concatenate([top, mid, low], axis=1).astype(BF16)
            y = jnp.dot(select, parts, preferred_element_type=F32)
            y = y[:, :n] + (y[:, n : 2 * n] + y[:, 2 * n :])
            gap[d] = y if c == 0 else gap[d] + y
    for c in range(chunks):
        wait_send(par_send[c], par_recv[c], 2 + chunks + c)


def body(node_coords, node_disp, qpoints, qweights, qcount, sec_block, pri_block):
    devices = lax.axis_size("gx") * lax.axis_size("gy")
    blocks, comps, n = node_coords.shape
    segs, _, points = qpoints.shape
    cap = 2 * segs // devices
    width = 2 * comps * n
    caps = [m * cap // sum(PHASES) for m in PHASES]
    kinds = 2 + 2 * len(caps)
    vmem, smem = pl.BlockSpec(memory_space=pltpu.VMEM), pl.BlockSpec(memory_space=pltpu.SMEM)
    gap = pl.pallas_call(
        fused_kernel,
        out_shape=jax.ShapeDtypeStruct((comps, blocks, n), F32),
        in_specs=[vmem, vmem, smem, vmem, vmem, vmem, vmem],
        out_specs=vmem,
        scratch_shapes=[
            pltpu.VMEM((devices, 1, 128), jnp.int32),
            pltpu.VMEM((devices, 1, 128), jnp.int32),
            pltpu.VMEM((devices, 128), F32),
            pltpu.SMEM((devices, 1, 128), jnp.int32),
            pltpu.VMEM((4, devices * cap), jnp.int32),
            pltpu.SMEM((4, devices * cap), jnp.int32),
            pltpu.VMEM((len(caps), devices * max(caps)), F32),
            pltpu.VMEM((devices, cap, width), F32),
            pltpu.VMEM((devices, cap, width), F32),
            pltpu.VMEM((segs, 8, points), F32),
            pltpu.VMEM((segs + 1, 8, n), F32),
            pltpu.VMEM((GROUP, 2 * n, points), BF16),
            pltpu.VMEM((GROUP, 8, points), F32),
            *[pltpu.VMEM((devices, m, width), F32) for m in caps + caps],
            *[pltpu.VMEM((devices, comps, m, n), F32) for m in caps + caps],
            pltpu.SemaphoreType.DMA((kinds, devices)),
            pltpu.SemaphoreType.DMA((kinds, devices)),
            pltpu.SemaphoreType.DMA((2,)),
        ],
        compiler_params=pltpu.CompilerParams(collective_id=0, has_side_effects=True),
        name="fused",
    )(
        pri_block, sec_block, qcount,
        node_coords.transpose(1, 0, 2), node_disp.transpose(1, 0, 2),
        qpoints.transpose(1, 0, 2), qweights,
    )
    return gap.transpose(1, 0, 2)


def solution(mesh):
    placed = (
        P(("gx", "gy"), None, None),
        P(("gx", "gy"), None, None),
        P(("gx", "gy"), None, None),
        P(("gx", "gy"), None),
        P(("gx", "gy")),
        P(("gx", "gy")),
        P(("gx", "gy")),
    )
    return jax.shard_map(
        body, mesh=mesh, in_specs=placed, out_specs=P(("gx", "gy"), None, None), check_vma=False
    )
```

time: 132 us -> 121 us (0.917)
  Pallas kernels: 109 us -> 119 us
  starting transfers between devices: 7.33 us -> 0 us
  waiting for transfers between devices: 5.95 us -> 0 us
  local copies, waits for them, and re-layouts: 5.99 us -> 1.92 us
  other arithmetic: 2.78 us -> 0 us
    pallas_call x1, Pallas kernels: 109 us -> 119 us  [body(): pl.pallas_call(fused_kernel, out_shape=jax.ShapeDtypeStruct((comps, block...]
    all_to_all x1 -> x0, starting transfers between devices: 7.33 us -> none  [exchange(): lax.all_to_all(x, ('gx', 'gy'), split_axis=0, concat_axis=0, tiled=True)]
    all_to_all x1 -> x0, waiting for transfers between devices: 5.95 us -> none  [exchange(): lax.all_to_all(x, ('gx', 'gy'), split_axis=0, concat_axis=0, tiled=True)]
    another operation x5 -> x0, local copies, waits for them, and re-layouts: 2.14 us -> none  [the longest x3 0.8 us: body(): jnp.stack([pri_request.reshape(devices, cap), sec_rows.reshape(devices, c...]
    reduce_sum x5 -> x0, other arithmetic: 1.45 us -> none  [the longest x3 1.05 us: pick(): jnp.sum(jnp.where(match, (values - empty)[:, None], 0), axis=0) + empty]
    unnamed x6 -> x1, local copies, waits for them, and re-layouts: 2.87 us -> 1.92 us
  transfers between devices with their start and end apart: 1 -> 0, of which waited for: 1 -> 0; matrix products, arithmetic and copies ran while one was open for 1% -> 0% of each run, Pallas kernels for 0% -> 0%
where the time goes in v2:
time: 121 us
  Pallas kernels  119 us (98%)
  local copies, waits for them, and re-layouts  1.92 us (2%)
    pallas_call x1, Pallas kernels, body(): pl.pallas_call(fused_kernel, out_shape=jax.ShapeDtypeStruct((comps, block...  119 us

profile of v2, /device:TPU:0, one launch (start us, length us, event | category | flops | bytes accessed | tf_op | source)
XLA Modules:
  0.0 120.8 jit_solution(2471098443948383113)
XLA Ops:
  0.0 118.8 %fused.1 = f32[3,384,128]{2,1,0:T(8,128)} custom-call(s32[256]{0:T(256)} %pri_block.1, s32[256]{0:T(256)} %sec_block.1, s32[256]{0:T(256)} %counts.1, f32[3,384,128]{2,1,0:T(8,128)} %bitcast.6, f32[3,384,128]{2,1,0:T(8,128)} %bitcast.7, f32[3,256,256]{2,1,0:T(8,128)} %bitcast.5, f32[256,256]{1,0:T(8,128)} %weights.1), custom_call_target="tpu_custom_call" | custom-call | tf_op jit(solution)/shard_map/fused/pallas_call | solution.py:373
  118.8 1.9 %copy.9 = f32[384,3,128]{2,0,1:T(8,128)} copy(f32[384,3,128]{2,0,1:T(8,128)} %bitcast.4) | data formatting | bytes 1179648

commit v3 on v2

--- a/solution.py
+++ b/solution.py
@@ -142,30 +142,38 @@
     quarter = cap // total
     firsts = [sum(PHASES[:c]) for c in range(chunks)]
     caps = [m * quarter for m in PHASES]
-    me = lax.axis_index("gx") * ny + lax.axis_index("gy")
+    nx = lax.axis_size("gx")
+    gx, gy = lax.axis_index("gx"), lax.axis_index("gy")
+    me = gx * ny + gy
+
+    def device(t):
+        far = lax.div(t, ny)
+        if nx & (nx - 1):
+            row = lax.rem(gx + far, nx)
+        else:
+            row, bit = 0, 1
+            while bit < nx:
+                row = row + bit * lax.rem(lax.div(gx, bit) + lax.div(far, bit), 2)
+                bit *= 2
+        return row, lax.rem(gy + t, ny)
 
     def partner(t):
-        return lax.rem(me + t, devices)
-
-    def device(p):
-        return (p // ny, lax.rem(p, ny))
+        row, column = device(t)
+        return row * ny + column
 
     def copy(src, dst, k, t):
-        p = partner(t)
+        row, column = device(t)
         return pltpu.make_async_remote_copy(
-            src_ref=src.at[p],
+            src_ref=src.at[row * ny + column],
             dst_ref=dst.at[me],
             send_sem=send_sem.at[k, t],
             recv_sem=recv_sem.at[k, t],
-            device_id=device(p),
+            device_id=(row, column),
             device_id_type=MESH,
         )
 
-    half = devices // 2
-
     def far_first(i):
-        t = i + half
-        return jnp.where(t >= devices, t - devices + 1, t)
+        return devices - 1 - i
 
     def fill_and_start(fill, src, dst, k):
         fill(partner(far_first(0)), src)
@@ -178,6 +186,18 @@
         fill(me, dst)
         copy(src, dst, k, far_first(devices - 2)).start()
 
+    def fill_all(fill, src, dst):
+        @pl.loop(1, devices)
+        def _(t):
+            fill(partner(t), src)
+
+        fill(me, dst)
+
+    def start_all(src, dst, k):
+        @pl.loop(0, devices - 1)
+        def _(i):
+            copy(src, dst, k, far_first(i)).start()
+
     def wait_recv(src, dst, k):
         @pl.loop(1, devices)
         def _(t):
@@ -192,7 +212,7 @@
 
     @pl.loop(1, devices)
     def _(t):
-        pl.semaphore_signal(barrier, inc=1, device_id=device(partner(t)), device_id_type=MESH)
+        pl.semaphore_signal(barrier, inc=1, device_id=device(t), device_id_type=MESH)
 
     pri = pri_block[...].reshape(1, segs).astype(F32)
     sec = sec_block[...].reshape(1, segs).astype(F32)
@@ -221,9 +241,7 @@
     req_recv[me] = whole(req_rows[pl.ds(me, 1), :], blocks)
     pl.semaphore_wait(barrier, devices - 1)
 
-    @pl.loop(0, devices - 1)
-    def _(i):
-        copy(req_send, req_recv, 0, far_first(i)).start()
+    start_all(req_send, req_recv, 0)
 
     number = lax.broadcasted_iota(jnp.int32, (1, segs), 1).astype(F32)
     zero = jnp.zeros((4, segs), F32)
@@ -263,7 +281,7 @@
     fill_and_start(functools.partial(gather, 0, cap), pri_send, pri_recv, 1)
     for c in range(chunks):
         fill = functools.partial(gather, cap + firsts[c] * quarter, caps[c])
-        fill_and_start(fill, sec_send[c], sec_recv[c], 2 + c)
+        fill_all(fill, sec_send[c], sec_recv[c])
 
     @pl.loop(0, devices)
     def _(p):
@@ -298,6 +316,7 @@
         return sums * inv, inv
 
     wait_recv(pri_send, pri_recv, 1)
+    start_all(sec_send[0], sec_recv[0], 2)
 
     @pl.loop(0, segs // GROUP)
     def _(i):
@@ -312,7 +331,13 @@
     steps = segs // total // GROUP
     for c in range(chunks):
         nodes = sec_recv[c]
+        if c == 0:
+            wait_send(req_send, req_recv, 0)
+            wait_send(pri_send, pri_recv, 1)
         wait_recv(sec_send[c], nodes, 2 + c)
+        if c == 0:
+            for later in range(1, chunks):
+                start_all(sec_send[later], sec_recv[later], 2 + later)
 
         @pl.loop(firsts[c] * steps, (firsts[c] + PHASES[c]) * steps)
         def _(i):
@@ -341,11 +366,12 @@
 
         fill_and_start(lift, par_send[c], par_recv[c], 2 + chunks + c)
 
-    wait_send(req_send, req_recv, 0)
-    wait_send(pri_send, pri_recv, 1)
     for c in range(chunks):
-        wait_send(sec_send[c], sec_recv[c], 2 + c)
-    for c in range(chunks):
+        if c == chunks - 1:
+            for k in range(chunks):
+                wait_send(sec_send[k], sec_recv[k], 2 + k)
+            for k in range(chunks - 1):
+                wait_send(par_send[k], par_recv[k], 2 + chunks + k)
         wait_recv(par_send[c], par_recv[c], 2 + chunks + c)
         size = devices * caps[c]
         row = lax.broadcasted_iota(jnp.int32, (blocks, size), 0).astype(F32)
@@ -357,8 +383,7 @@
             y = jnp.dot(select, parts, preferred_element_type=F32)
             y = y[:, :n] + (y[:, n : 2 * n] + y[:, 2 * n :])
             gap[d] = y if c == 0 else gap[d] + y
-    for c in range(chunks):
-        wait_send(par_send[c], par_recv[c], 2 + chunks + c)
+    wait_send(par_send[-1], par_recv[-1], 1 + 2 * chunks)
 
 
 def body(node_coords, node_disp, qpoints, qweights, qcount, sec_block, pri_block):

time: 121 us -> 111 us (0.917)
  Pallas kernels: 119 us -> 109 us
    pallas_call x1, Pallas kernels: 119 us -> 109 us  [body(): pl.pallas_call(fused_kernel, out_shape=jax.ShapeDtypeStruct((comps, block...]
where the time goes in v3:
time: 111 us
  Pallas kernels  109 us (98%)
  local copies, waits for them, and re-layouts  1.92 us (2%)
    pallas_call x1, Pallas kernels, body(): pl.pallas_call(fused_kernel, out_shape=jax.ShapeDtypeStruct((comps, block...  109 us

profile of v3, /device:TPU:0, one launch (start us, length us, event | category | flops | bytes accessed | tf_op | source)
XLA Modules:
  0.0 111.3 jit_solution(1359829086883673204)
XLA Ops:
  0.0 109.4 %fused.1 = f32[3,384,128]{2,1,0:T(8,128)} custom-call(s32[256]{0:T(256)} %pri_block.1, s32[256]{0:T(256)} %sec_block.1, s32[256]{0:T(256)} %counts.1, f32[3,384,128]{2,1,0:T(8,128)} %bitcast.6, f32[3,384,128]{2,1,0:T(8,128)} %bitcast.7, f32[3,256,256]{2,1,0:T(8,128)} %bitcast.5, f32[256,256]{1,0:T(8,128)} %weights.1), custom_call_target="tpu_custom_call" | custom-call | tf_op jit(solution)/shard_map/fused/pallas_call | solution.py:398
  109.4 1.9 %copy.9 = f32[384,3,128]{2,0,1:T(8,128)} copy(f32[384,3,128]{2,0,1:T(8,128)} %bitcast.4) | data formatting | bytes 1179648

commit v4 on v3

--- a/solution.py
+++ b/solution.py
@@ -122,8 +122,8 @@
 
 
 def fused_kernel(
-    pri_block, sec_block, counts, coords, disp, qp, weights, gap,
-    req_send, req_recv, req_rows, ids, table_v, table, hot,
+    pri_block, sec_block, counts, coords_h, disp_h, qp_h, weights_h, gap,
+    coords, disp, qp, weights, req_send, req_recv, req_rows, ids, table_v, table, hot,
     pri_send, pri_recv, means, parcels, both_s, gap_s, *rest,
 ):
     chunks = len(PHASES)
@@ -166,8 +166,8 @@
         return pltpu.make_async_remote_copy(
             src_ref=src.at[row * ny + column],
             dst_ref=dst.at[me],
-            send_sem=send_sem.at[k, t],
-            recv_sem=recv_sem.at[k, t],
+            send_sem=send_sem.at[k],
+            recv_sem=recv_sem.at[k],
             device_id=(row, column),
             device_id_type=MESH,
         )
@@ -198,16 +198,31 @@
         def _(i):
             copy(src, dst, k, far_first(i)).start()
 
+    def all_of(src, dst, k):
+        row, column = device(1)
+        return pltpu.make_async_remote_copy(
+            src_ref=src.at[pl.ds(0, devices - 1)],
+            dst_ref=dst.at[pl.ds(0, devices - 1)],
+            send_sem=send_sem.at[k],
+            recv_sem=recv_sem.at[k],
+            device_id=(row, column),
+            device_id_type=MESH,
+        )
+
     def wait_recv(src, dst, k):
-        @pl.loop(1, devices)
-        def _(t):
-            copy(src, dst, k, t).wait_recv()
+        all_of(src, dst, k).wait_recv()
 
     def wait_send(src, dst, k):
-        @pl.loop(1, devices)
-        def _(t):
-            copy(src, dst, k, t).wait_send()
-
+        all_of(src, dst, k).wait_send()
+
+    loads = [
+        pltpu.make_async_copy(src, dst, local_sem.at[2 + i])
+        for i, (src, dst) in enumerate(
+            [(coords_h, coords), (disp_h, disp), (qp_h, qp), (weights_h, weights)]
+        )
+    ]
+    for load in loads:
+        load.start()
     barrier = pltpu.get_barrier_semaphore()
 
     @pl.loop(1, devices)
@@ -267,6 +282,8 @@
     wait_recv(req_send, req_recv, 0)
     load_ids = pltpu.make_async_copy(req_recv, ids, local_sem.at[1])
     load_ids.start()
+    for load in loads:
+        load.wait()
     load_table.wait()
     load_ids.wait()
 
@@ -397,10 +414,14 @@
     vmem, smem = pl.BlockSpec(memory_space=pltpu.VMEM), pl.BlockSpec(memory_space=pltpu.SMEM)
     gap = pl.pallas_call(
         fused_kernel,
-        out_shape=jax.ShapeDtypeStruct((comps, blocks, n), F32),
-        in_specs=[vmem, vmem, smem, vmem, vmem, vmem, vmem],
+        out_shape=pltpu.VMEM((comps, blocks, n), F32),
+        in_specs=[vmem, vmem, smem] + [pl.BlockSpec(memory_space=pltpu.HBM)] * 4,
         out_specs=vmem,
         scratch_shapes=[
+            pltpu.VMEM((comps, blocks, n), F32),
+            pltpu.VMEM((comps, blocks, n), F32),
+            pltpu.VMEM((comps, segs, points), F32),
+            pltpu.VMEM((segs, points), F32),
             pltpu.VMEM((devices, 1, 128), jnp.int32),
             pltpu.VMEM((devices, 1, 128), jnp.int32),
             pltpu.VMEM((devices, 128), F32),
@@ -416,9 +437,9 @@
             pltpu.VMEM((GROUP, 8, points), F32),
             *[pltpu.VMEM((devices, m, width), F32) for m in caps + caps],
             *[pltpu.VMEM((devices, comps, m, n), F32) for m in caps + caps],
-            pltpu.SemaphoreType.DMA((kinds, devices)),
-            pltpu.SemaphoreType.DMA((kinds, devices)),
-            pltpu.SemaphoreType.DMA((2,)),
+            pltpu.SemaphoreType.DMA((kinds,)),
+            pltpu.SemaphoreType.DMA((kinds,)),
+            pltpu.SemaphoreType.DMA((6,)),
         ],
         compiler_params=pltpu.CompilerParams(collective_id=0, has_side_effects=True),
         name="fused",

time: 111 us -> 104 us (0.937)
  Pallas kernels: 109 us -> 103 us
    pallas_call x1, Pallas kernels: 109 us -> 103 us  [body(): pl.pallas_call(fused_kernel, out_shape=pltpu.VMEM((comps, blocks, n), F32...]
where the time goes in v4:
time: 104 us
  Pallas kernels  103 us (99%)
    pallas_call x1, Pallas kernels, body(): pl.pallas_call(fused_kernel, out_shape=pltpu.VMEM((comps, blocks, n), F32...  103 us

profile of v4, /device:TPU:0, one launch (start us, length us, event | category | flops | bytes accessed | tf_op | source)
XLA Modules:
  0.0 104.0 jit_solution(13279195566029397382)
XLA Ops:
  0.0 103.1 %fused.1 = f32[3,384,128]{2,1,0:T(8,128)S(1)} custom-call(s32[256]{0:T(256)} %pri_block.1, s32[256]{0:T(256)} %sec_block.1, s32[256]{0:T(256)} %counts.1, f32[3,384,128]{2,1,0:T(8,128)} %bitcast.6, f32[3,384,128]{2,1,0:T(8,128)} %bitcast.7, f32[3,256,256]{2,1,0:T(8,128)} %bitcast.5, f32[256,256]{1,0:T(8,128)} %weights_h.1), custom_call_target="tpu_custom_call" | custom-call | tf_op jit(solution)/shard_map/fused/pallas_call | solution.py:415
  103.1 0.8 copy.9

commit v5 on v4

--- a/solution.py
+++ b/solution.py
@@ -123,7 +123,7 @@
 
 def fused_kernel(
     pri_block, sec_block, counts, coords_h, disp_h, qp_h, weights_h, gap,
-    coords, disp, qp, weights, req_send, req_recv, req_rows, ids, table_v, table, hot,
+    coords, disp, qp, weights, feats, req_send, req_recv, req_rows, ids, table_v, table, hot,
     pri_send, pri_recv, means, parcels, both_s, gap_s, *rest,
 ):
     chunks = len(PHASES)
@@ -225,9 +225,11 @@
         load.start()
     barrier = pltpu.get_barrier_semaphore()
 
-    @pl.loop(1, devices)
-    def _(t):
-        pl.semaphore_signal(barrier, inc=1, device_id=device(t), device_id_type=MESH)
+    @pl.loop(0, devices - 1)
+    def _(i):
+        pl.semaphore_signal(
+            barrier, inc=1, device_id=device(far_first(i)), device_id_type=MESH
+        )
 
     pri = pri_block[...].reshape(1, segs).astype(F32)
     sec = sec_block[...].reshape(1, segs).astype(F32)
@@ -320,9 +322,9 @@
     def row_of(nodes, spot):
         return nodes[spot // nodes.shape[1], pl.ds(lax.rem(spot, nodes.shape[1]), 1), :]
 
-    def group_values(nodes, slot_of, seg_of):
+    def group_values(nodes, slot_of, feat_of):
         for g in range(GROUP):
-            kh, kl = kernel_values(row_of(nodes, slot_of(g)), point_features(qp, seg_of(g)), n)
+            kh, kl = kernel_values(row_of(nodes, slot_of(g)), feat_of(g), n)
             both_s[g, :n] = kh
             both_s[g, n:] = kl
 
@@ -337,7 +339,12 @@
 
     @pl.loop(0, segs // GROUP)
     def _(i):
-        group_values(pri_recv, lambda g: table[0, i * GROUP + g], lambda g: i * GROUP + g)
+        def fresh(g):
+            feat = point_features(qp, i * GROUP + g)
+            feats[i * GROUP + g] = feat
+            return feat
+
+        group_values(pri_recv, lambda g: table[0, i * GROUP + g], fresh)
         for g in range(GROUP):
             s = i * GROUP + g
             means[s] = mean_of(row_of(pri_recv, table[0, s]), g)[0]
@@ -358,7 +365,7 @@
 
         @pl.loop(firsts[c] * steps, (firsts[c] + PHASES[c]) * steps)
         def _(i):
-            group_values(nodes, lambda g: table[2, i * GROUP + g], lambda g: table[1, i * GROUP + g])
+            group_values(nodes, lambda g: table[2, i * GROUP + g], lambda g: feats[table[1, i * GROUP + g]])
             for g in range(GROUP):
                 s = table[1, i * GROUP + g]
                 mean, inv = mean_of(row_of(nodes, table[2, i * GROUP + g]), g)
@@ -422,6 +429,7 @@
             pltpu.VMEM((comps, blocks, n), F32),
             pltpu.VMEM((comps, segs, points), F32),
             pltpu.VMEM((segs, points), F32),
+            pltpu.VMEM((segs, 48, points), BF16),
             pltpu.VMEM((devices, 1, 128), jnp.int32),
             pltpu.VMEM((devices, 1, 128), jnp.int32),
             pltpu.VMEM((devices, 128), F32),

time: 104 us -> 103 us (level)
  no operation moved by 1% of the time
where the time goes in v5:
time: 103 us
  Pallas kernels  103 us (100%)
    pallas_call x1, Pallas kernels, body(): pl.pallas_call(fused_kernel, out_shape=pltpu.VMEM((comps, blocks, n), F32...  103 us

profile of v5, /device:TPU:0, one launch (start us, length us, event | category | flops | bytes accessed | tf_op | source)
XLA Modules:
  0.0 103.3 jit_solution(2705362099185882327)
XLA Ops:
  0.0 102.5 %fused.1 = f32[3,384,128]{2,1,0:T(8,128)S(1)} custom-call(s32[256]{0:T(256)} %pri_block.1, s32[256]{0:T(256)} %sec_block.1, s32[256]{0:T(256)} %counts.1, f32[3,384,128]{2,1,0:T(8,128)} %bitcast.6, f32[3,384,128]{2,1,0:T(8,128)} %bitcast.7, f32[3,256,256]{2,1,0:T(8,128)} %bitcast.5, f32[256,256]{1,0:T(8,128)} %weights_h.1), custom_call_target="tpu_custom_call" | custom-call | tf_op jit(solution)/shard_map/fused/pallas_call | solution.py:422
  102.5 0.8 copy.9
